TPU v7x, 32 devices: a whole 2x2x4 slice. The times are simulated.
32 devices in a mesh: lat: 4 (over z), lon: 8 (over y, x, core).
Axes of the slice: x: 2, y: 2, z: 4, core: 2. Of those that a mesh axis runs over, the one named last changes fastest.
Arguments:
- grid_latent: bfloat16 [16384, 512], P(('lat', 'lon')), may hold values from -6 to 6
- mesh_latent: bfloat16 [4096, 512], P(('lat', 'lon')), may hold values from -6 to 6
- block_weights: bfloat16 [4, 3, 512, 512], replicated, may hold values from -0.25 to 0.25
- block_gains: float32 [4, 512], replicated, may hold values from 0.5 to 1.5
- grid_cot: bfloat16 [16384, 512], P(('lat', 'lon')), may hold values from -0.046875 to 0.046875
- encode_rows: int32 [32, 32, 4], P(('lat', 'lon')), may hold values from 0 to 511
- encode_senders: int32 [32, 1536], P(('lat', 'lon')), may hold values from 0 to 127, as said below
- encode_receivers: int32 [32, 1536], P(('lat', 'lon')), may hold values from 0 to 127, as said below
- encode_blocks: int32 [32], P(('lat', 'lon')), may hold values from 4 to 12, as said below
- process_rows: int32 [32, 32, 4], P(('lat', 'lon')), may hold values from 0 to 127
- process_senders: int32 [32, 1536], P(('lat', 'lon')), may hold values from 0 to 127, as said below
- process_receivers: int32 [32, 1536], P(('lat', 'lon')), may hold values from 0 to 127, as said below
- process_blocks: int32 [32], P(('lat', 'lon')), may hold values from 4 to 12, as said below
- decode_rows: int32 [32, 32, 4], P(('lat', 'lon')), may hold values from 0 to 127
- decode_senders: int32 [32, 1536], P(('lat', 'lon')), may hold values from 0 to 127, as said below
- decode_receivers: int32 [32, 1536], P(('lat', 'lon')), may hold values from 0 to 511, as said below
- decode_blocks: int32 [32], P(('lat', 'lon')), may hold values from 4 to 12, as said below
Outputs:
- grid_out: bfloat16 [16384, 512], P(('lat', 'lon'))
- weight_grad: bfloat16 [4, 3, 512, 512], replicated
- gain_grad: float32 [4, 512], replicated
Inputs may be any that keep to these rules, and one draw needn't show every extreme that they name: `encode_senders`: on every device each of the 128 received slots is named by some edge of the first 4 blocks. `encode_receivers`: on every device each of its 128 mesh rows is named by some edge of the first 4 blocks. `encode_blocks`: some device has 12 live blocks. `process_senders`: on every device each of the 128 received slots is named by some edge of the first 4 blocks. `process_receivers`: on every device each of its 128 mesh rows is named by some edge of the first 4 blocks. `process_blocks`: some device has 12 live blocks. `decode_senders`: on every device each of the 128 received slots is named by some edge of the first 4 blocks. `decode_receivers`: on every device each of its 512 grid rows is named by some edge of the first 4 blocks. `decode_blocks`: some device has 12 live blocks.
All inputs are finite; a program needn't handle non-finite values.
Results may differ from a plain program's by a relative error of at most 0.017.
Values may be sent and summed in bfloat16 or wider, within the bound.
No kernel may reach another device: no remote copies, remote signals or barrier semaphores. Data moves between devices by JAX's collectives and lax.ppermute only.
A program may use at most 128 MiB of HBM per device.

v0:
```python
import jax
import jax.numpy as jnp
from jax import lax
from jax.sharding import PartitionSpec as P

LAYERS = 2
EDGE_BLOCK = 128
EPSILON = 1e-05


def silu_slope(values):
    sigma = jax.nn.sigmoid(values)
    return sigma * (1.0 + values * (1.0 - sigma))


def transposed_product(left, right):
    return lax.dot_general(
        left, right, (((0,), (0,)), ((), ())), preferred_element_type=jnp.float32
    )


def back_product(grad, weight):
    return lax.dot_general(
        grad, weight, (((1,), (1,)), ((), ())), preferred_element_type=jnp.float32
    )


def projected(latent, weight):
    return jnp.dot(latent, weight, preferred_element_type=jnp.float32).astype(jnp.bfloat16)


def edge_forward(
    slot_vals, proj_recv, latent_recv, senders, receivers, live_mask, weight_out, block_gain
):
    preact = slot_vals[senders].astype(jnp.float32) + proj_recv[receivers].astype(jnp.float32)
    hidden = jax.nn.silu(preact) * live_mask[:, None]
    summed = jax.ops.segment_sum(hidden, receivers, num_segments=proj_recv.shape[0]).astype(
        jnp.bfloat16
    )
    mixed = jnp.dot(summed, weight_out, preferred_element_type=jnp.float32)
    centred = mixed - jnp.mean(mixed, axis=-1, keepdims=True)
    inv_scale = lax.rsqrt(jnp.mean(centred * centred, axis=-1, keepdims=True) + EPSILON)
    normed = centred * inv_scale
    output = (latent_recv.astype(jnp.float32) + normed * block_gain).astype(jnp.bfloat16)
    return (output, preact, summed, normed, inv_scale)


def edge_backward(
    grad_out,
    preact,
    summed,
    normed,
    inv_scale,
    senders,
    receivers,
    live_mask,
    weight_out,
    block_gain,
    recv_count,
    slot_count,
):
    gain_part = jnp.sum(grad_out * normed, axis=0)
    grad_normed = grad_out * block_gain
    grad_mixed = inv_scale * (
        grad_normed
        - jnp.mean(grad_normed, axis=-1, keepdims=True)
        - normed * jnp.mean(grad_normed * normed, axis=-1, keepdims=True)
    )
    grad_mixed = grad_mixed.astype(jnp.bfloat16)
    out_part = transposed_product(summed, grad_mixed)
    grad_summed = back_product(grad_mixed, weight_out)
    grad_pre = grad_summed[receivers] * live_mask[:, None] * silu_slope(preact)
    grad_recv = jax.ops.segment_sum(grad_pre, receivers, num_segments=recv_count).astype(
        jnp.bfloat16
    )
    grad_slots = jax.ops.segment_sum(grad_pre, senders, num_segments=slot_count).astype(
        jnp.bfloat16
    )
    return (grad_recv, grad_slots, out_part, gain_part)


def trade(buffer):
    return lax.all_to_all(buffer, ("lat", "lon"), split_axis=0, concat_axis=0, tiled=True)


def graph_parts(send_rows, senders, receivers, block_count):
    positions = jnp.arange(senders.shape[1], dtype=jnp.int32) // EDGE_BLOCK
    live_mask = (positions < block_count[0]).astype(jnp.float32)
    return (send_rows[0], senders[0], receivers[0], live_mask)


def run_forward(latent_send, latent_recv, weights, block_gain, graph):
    send_rows, senders, receivers, live_mask = graph
    proj_send = projected(latent_send, weights[0])
    outgoing = proj_send[send_rows]
    proj_recv = projected(latent_recv, weights[1])
    slot_vals = trade(outgoing).reshape(-1, proj_send.shape[1])
    output, preact, summed, normed, inv_scale = edge_forward(
        slot_vals, proj_recv, latent_recv, senders, receivers, live_mask, weights[2], block_gain
    )
    return (output, (preact, summed, normed, inv_scale, slot_vals.shape[0]))


def run_backward(grad_out, latent_send, latent_recv, weights, block_gain, graph, saved):
    send_rows, senders, receivers, live_mask = graph
    preact, summed, normed, inv_scale, slot_count = saved
    grad_recv, grad_slots, out_part, gain_part = edge_backward(
        grad_out,
        preact,
        summed,
        normed,
        inv_scale,
        senders,
        receivers,
        live_mask,
        weights[2],
        block_gain,
        latent_recv.shape[0],
        slot_count,
    )
    width = grad_slots.shape[1]
    returned = trade(grad_slots.reshape(send_rows.shape + (width,)))
    grad_send = (
        jnp.zeros((latent_send.shape[0], width), jnp.float32)
        .at[send_rows.reshape(-1)]
        .add(returned.reshape(-1, width).astype(jnp.float32))
        .astype(jnp.bfloat16)
    )
    grad_weights = jnp.stack(
        [
            transposed_product(latent_send, grad_send),
            transposed_product(latent_recv, grad_recv),
            out_part,
        ]
    )
    return (grad_weights, gain_part, grad_send, grad_recv)


def settle(grad_weights, gain_part):
    return (grad_weights, gain_part)


def shards(
    grid_latent,
    mesh_latent,
    block_weights,
    block_gains,
    grid_cot,
    encode_rows,
    encode_senders,
    encode_receivers,
    encode_blocks,
    process_rows,
    process_senders,
    process_receivers,
    process_blocks,
    decode_rows,
    decode_senders,
    decode_receivers,
    decode_blocks,
):
    encode = graph_parts(encode_rows, encode_senders, encode_receivers, encode_blocks)
    process = graph_parts(process_rows, process_senders, process_receivers, process_blocks)
    decode = graph_parts(decode_rows, decode_senders, decode_receivers, decode_blocks)
    latents = [mesh_latent]
    saves = []
    output, saved = run_forward(grid_latent, mesh_latent, block_weights[0], block_gains[0], encode)
    latents.append(output)
    saves.append(saved)
    for layer_id in range(LAYERS):
        current = latents[-1]
        output, saved = run_forward(
            current, current, block_weights[layer_id + 1], block_gains[layer_id + 1], process
        )
        latents.append(output)
        saves.append(saved)
    last_id = LAYERS + 1
    grid_out, decode_saved = run_forward(
        latents[-1], grid_latent, block_weights[last_id], block_gains[last_id], decode
    )
    weight_parts = [None] * (LAYERS + 2)
    gain_parts = [None] * (LAYERS + 2)
    grad_weights, gain_part, grad_send, grad_recv = run_backward(
        grid_cot.astype(jnp.float32),
        latents[-1],
        grid_latent,
        block_weights[last_id],
        block_gains[last_id],
        decode,
        decode_saved,
    )
    weight_parts[last_id], gain_parts[last_id] = settle(grad_weights, gain_part)
    grad_mesh = back_product(grad_send, block_weights[last_id][0])
    for layer_id in reversed(range(LAYERS)):
        block_id = layer_id + 1
        current = latents[block_id]
        grad_weights, gain_part, grad_send, grad_recv = run_backward(
            grad_mesh,
            current,
            current,
            block_weights[block_id],
            block_gains[block_id],
            process,
            saves[block_id],
        )
        weight_parts[block_id], gain_parts[block_id] = settle(grad_weights, gain_part)
        grad_mesh = (
            grad_mesh
            + back_product(grad_recv, block_weights[block_id][1])
            + back_product(grad_send, block_weights[block_id][0])
        )
    grad_weights, gain_part, grad_send, grad_recv = run_backward(
        grad_mesh, grid_latent, mesh_latent, block_weights[0], block_gains[0], encode, saves[0]
    )
    weight_parts[0], gain_parts[0] = settle(grad_weights, gain_part)
    weight_stack = jnp.stack(weight_parts)
    gain_stack = jnp.stack(gain_parts)
    weight_stack, gain_stack = lax.psum((weight_stack, gain_stack), ("lat", "lon"))
    return (grid_out, weight_stack.astype(jnp.bfloat16), gain_stack)


def solution(mesh):
    return jax.shard_map(
        shards,
        mesh=mesh,
        in_specs=(
            P(("lat", "lon"), None),
            P(("lat", "lon"), None),
            P(),
            P(),
            P(("lat", "lon"), None),
            P(("lat", "lon"), None, None),
            P(("lat", "lon"), None),
            P(("lat", "lon"), None),
            P(("lat", "lon")),
            P(("lat", "lon"), None, None),
            P(("lat", "lon"), None),
            P(("lat", "lon"), None),
            P(("lat", "lon")),
            P(("lat", "lon"), None, None),
            P(("lat", "lon"), None),
            P(("lat", "lon"), None),
            P(("lat", "lon")),
        ),
        out_specs=(P(("lat", "lon"), None), P(), P()),
        check_vma=False,
    )
```

profile of v0, /device:TPU:0, one launch (start us, length us, event | category | flops | bytes accessed | tf_op | source)
XLA Modules:
  0.0 602.4 jit_solution(12311952505016923633)
XLA Ops:
  4.9 7.3 %all-to-all-start = ((bf16[32,4,512]{2,1,0:T(4,128)(2,1)}), bf16[32,4,512]{2,1,0:T(4,128)(2,1)S(1)}, u32[]{:S(2)}, u32[]{:S(2)}) async-start(bf16[32,4,512]{2,1,0:T(4,128)(2,1)} %reshape.518), calls=%async_computation | async-start | bytes 262144 | tf_op jit(solution)/shard_map/all_to_all | solution.py:83
  31.2 11.8 %scatter_custom_fusion = f32[128,512]{1,0:T(8,128)S(1)} fusion(s32[1536]{0:T(1024)S(1)} %reduce.1, bf16[1536,512]{1,0:T(8,128)(2,1)S(1)} %gather_fusion.2, bf16[1536,512]{1,0:T(8,128)(2,1)} %gather_fusion.1, f32[1536]{0:T(1024)S(1)} %fusion.133, f32[]{:T(128)} %constant.63.clone.1, f32[]{:T(128)} %constant.59.clone.1), kind=kCustom, calls=%fused_computation.56 | custom fusion | flops 7077888 | bytes 3416072 | tf_op jit(solution)/shard_map/scatter-add | solution.py:37
  48.3 5.8 all-to-all-start.1
  56.2 5.4 gather_fusion.5
  67.8 11.9 %scatter_custom_fusion.1 = f32[128,512]{1,0:T(8,128)S(1)} fusion(s32[1536]{0:T(1024)S(1)} %reduce.4, bf16[1536,512]{1,0:T(8,128)(2,1)} %gather_fusion.5, bf16[1536,512]{1,0:T(8,128)(2,1)} %gather_fusion.4, f32[1536]{0:T(1024)S(1)} %fusion.134, f32[]{:T(128)} %constant.63.clone.1, f32[]{:T(128)} %constant.59.clone.1), kind=kCustom, calls=%fused_computation.51 | custom fusion | flops 7077888 | bytes 3416072 | tf_op jit(solution)/shard_map/scatter-add | solution.py:37
  92.0 5.4 gather_fusion.8
  98.4 5.4 gather_fusion.7
  103.8 11.7 %scatter_custom_fusion.2 = f32[128,512]{1,0:T(8,128)S(1)} fusion(s32[1536]{0:T(1024)S(1)} %reduce.4, bf16[1536,512]{1,0:T(8,128)(2,1)} %gather_fusion.8, bf16[1536,512]{1,0:T(8,128)(2,1)} %gather_fusion.7, f32[1536]{0:T(1024)S(1)} %fusion.134, f32[]{:T(128)} %constant.63.clone.1, f32[]{:T(128)} %constant.59.clone.1), kind=kCustom, calls=%fused_computation.46 | custom fusion | flops 7077888 | bytes 3416072 | tf_op jit(solution)/shard_map/scatter-add | solution.py:37
  136.2 5.4 gather_fusion.11
  142.3 5.7 gather_fusion.10
  148.0 13.0 %scatter_custom_fusion.3 = f32[512,512]{1,0:T(8,128)} fusion(s32[1536]{0:T(1024)} %reduce, bf16[1536,512]{1,0:T(8,128)(2,1)S(1)} %copy-done.3, bf16[1536,512]{1,0:T(8,128)(2,1)} %gather_fusion.10, f32[1536]{0:T(1024)} %fusion.135, f32[]{:T(128)} %constant.63.clone.1, f32[]{:T(128)} %constant.59.clone.1), kind=kCustom, calls=%fused_computation.41 | custom fusion | flops 7077888 | bytes 4203520 | tf_op jit(solution)/shard_map/scatter-add | solution.py:37
  177.0 11.0 %scatter_custom_fusion.4 = f32[128,512]{1,0:T(8,128)} fusion(s32[1536]{0:T(1024)} %reduce.10, f32[1536,512]{1,0:T(8,128)} %multiply_multiply_fusion.3, f32[]{:T(128)} %constant.59.clone.1), kind=kCustom, calls=%fused_computation.206 | custom fusion | flops 786432 | bytes 262656 | tf_op jit(solution)/shard_map/scatter-add | solution.py:76
  189.7 5.8 all-to-all-start.4
  198.1 10.5 %scatter_custom_fusion.15 = f32[512,512]{1,0:T(8,128)S(1)} fusion(s32[1536]{0:T(1024)} %reduce, f32[1536,512]{1,0:T(8,128)} %multiply_multiply_fusion.3, f32[]{:T(128)} %constant.59.clone.1), kind=kCustom, calls=%fused_computation.141 | custom fusion | flops 786432 | bytes 1049088 | tf_op jit(solution)/shard_map/scatter-add | solution.py:73
  230.3 10.4 %scatter_custom_fusion.6 = f32[128,512]{1,0:T(8,128)S(1)} fusion(s32[1536]{0:T(1024)} %copy-done.68, f32[1536,512]{1,0:T(8,128)} %multiply_multiply_fusion.2, f32[]{:T(128)} %constant.59.clone.1), kind=kCustom, calls=%fused_computation.202 | custom fusion | flops 786432 | bytes 262656 | tf_op jit(solution)/shard_map/scatter-add | solution.py:73
  240.7 10.3 %scatter_custom_fusion.7 = f32[128,512]{1,0:T(8,128)S(1)} fusion(s32[1536]{0:T(1024)} %reduce.11, f32[1536,512]{1,0:T(8,128)} %multiply_multiply_fusion.2, f32[]{:T(128)} %constant.59.clone.1), kind=kCustom, calls=%fused_computation.200 | custom fusion | flops 786432 | bytes 262656 | tf_op jit(solution)/shard_map/scatter-add | solution.py:76
  251.7 6.0 all-to-all-start.5
  284.4 10.4 %scatter_custom_fusion.9 = f32[128,512]{1,0:T(8,128)S(1)} fusion(s32[1536]{0:T(1024)} %copy-done.68, f32[1536,512]{1,0:T(8,128)} %multiply_multiply_fusion.1, f32[]{:T(128)} %constant.59.clone.1), kind=kCustom, calls=%fused_computation.196 | custom fusion | flops 786432 | bytes 262656 | tf_op jit(solution)/shard_map/scatter-add | solution.py:73
  294.8 10.3 %scatter_custom_fusion.10 = f32[128,512]{1,0:T(8,128)S(1)} fusion(s32[1536]{0:T(1024)} %reduce.11, f32[1536,512]{1,0:T(8,128)} %multiply_multiply_fusion.1, f32[]{:T(128)} %constant.59.clone.1), kind=kCustom, calls=%fused_computation.194 | custom fusion | flops 786432 | bytes 262656 | tf_op jit(solution)/shard_map/scatter-add | solution.py:76
  336.4 10.5 %scatter_custom_fusion.14 = f32[128,512]{1,0:T(8,128)S(1)} fusion(s32[1536]{0:T(1024)} %copy-done.67, f32[1536,512]{1,0:T(8,128)} %multiply_multiply_fusion, f32[]{:T(128)} %constant.59.clone.1), kind=kCustom, calls=%fused_computation.188 | custom fusion | flops 786432 | bytes 262656 | tf_op jit(solution)/shard_map/scatter-add | solution.py:73
  346.9 10.3 %scatter_custom_fusion.12 = f32[128,512]{1,0:T(8,128)S(1)} fusion(s32[1536]{0:T(1024)} %reduce.9, f32[1536,512]{1,0:T(8,128)} %multiply_multiply_fusion, f32[]{:T(128)} %constant.59.clone.1), kind=kCustom, calls=%fused_computation.190 | custom fusion | flops 786432 | bytes 262656 | tf_op jit(solution)/shard_map/scatter-add | solution.py:76
  375.9 6.6 %pad_maximum_fusion = f32[4,3,512,512]{2,3,1,0:T(8,128)} fusion(f32[1,3,512,512]{2,3,1,0:T(8,128)S(1)} %copy-done.4, f32[1,3,512,512]{2,3,1,0:T(8,128)S(1)} %copy-done.5, f32[1,3,512,512]{2,3,1,0:T(8,128)} %maximum_bitcast_fusion.1, f32[1,3,512,512]{2,3,1,0:T(8,128)S(1)} %maximum_bitcast_fusion), kind=kLoop, calls=%fused_computation.32 | loop fusion | flops 9437184 | bytes 25165824 | tf_op jit(solution)/shard_map/stack | solution.py:216
  382.5 210.8 %all-reduce.2 = (bf16[4,3,512,512]{2,3,1,0:T(8,128)(2,1)}, f32[4,512]{1,0:T(4,128)}) all-reduce(f32[4,3,512,512]{2,3,1,0:T(8,128)} %pad_maximum_fusion, f32[4,512]{1,0:T(4,128)S(1)} %pad_maximum_fusion.1), channel_id=1, replica_groups=mesh['lat'=4,'lon'=8] {'lat','lon'}, use_global_device_ids=true, to_apply=%region_32.33 | all-reduce | flops 3147776 | bytes 18890752 | tf_op jit(solution)/shard_map/psum | solution.py:218
  593.3 8.6 %copy.57 = bf16[4,3,512,512]{3,2,1,0:T(8,128)(2,1)} copy(bf16[4,3,512,512]{2,3,1,0:T(8,128)(2,1)} %get-tuple-element.21) | data formatting | bytes 12582912
  (318 shorter events, 187.6 us)
Async XLA Ops:
  4.9 20.8 %all-to-all-start = ((bf16[32,4,512]{2,1,0:T(4,128)(2,1)}), bf16[32,4,512]{2,1,0:T(4,128)(2,1)S(1)}, u32[]{:S(2)}, u32[]{:S(2)}) async-start(bf16[32,4,512]{2,1,0:T(4,128)(2,1)} %reshape.518), calls=%async_computation | async-start | bytes 262144 | tf_op jit(solution)/shard_map/all_to_all | solution.py:83
  16.6 28.1 %copy-start.48 = (f32[1,512]{1,0:T(1,128)}, f32[1,512]{1,0:T(1,128)S(1)}, u32[]{:S(2)}) copy-start(f32[1,512]{1,0:T(1,128)S(1)} %get-tuple-element.27) | copy-start | bytes 6148
  16.6 64.8 %copy-start.50 = (f32[1,512]{1,0:T(1,128)}, f32[1,512]{1,0:T(1,128)S(1)}, u32[]{:S(2)}) copy-start(f32[1,512]{1,0:T(1,128)S(1)} %get-tuple-element.26) | copy-start | bytes 6148
  45.4 36.0 %copy-start.33 = (bf16[128,512]{1,0:T(8,128)(2,1)}, bf16[128,512]{1,0:T(8,128)(2,1)S(1)}, u32[]{:S(2)}) copy-start(bf16[128,512]{1,0:T(8,128)(2,1)S(1)} %add_convert_fusion.3) | copy-start | bytes 393220
  48.3 14.0 %all-to-all-start.1 = ((bf16[32,4,512]{2,1,0:T(4,128)(2,1)}), bf16[32,4,512]{2,1,0:T(4,128)(2,1)S(1)}, u32[]{:S(2)}, u32[]{:S(2)}) async-start(bf16[32,4,512]{2,1,0:T(4,128)(2,1)} %reshape.542), calls=%async_computation.1 | async-start | bytes 262144 | tf_op jit(solution)/shard_map/all_to_all | solution.py:83
  54.7 49.1 %copy-start.68 = (s32[1536]{0:T(1024)}, s32[1536]{0:T(1024)S(1)}, u32[]{:S(2)}) copy-start(s32[1536]{0:T(1024)S(1)} %reduce.4) | copy-start | bytes 18436
  82.1 35.1 %copy-start.35 = (bf16[128,512]{1,0:T(8,128)(2,1)}, bf16[128,512]{1,0:T(8,128)(2,1)S(1)}, u32[]{:S(2)}) copy-start(bf16[128,512]{1,0:T(8,128)(2,1)S(1)} %add_convert_fusion.2) | copy-start | bytes 393220
  85.0 13.4 %all-to-all-start.2 = ((bf16[32,4,512]{2,1,0:T(4,128)(2,1)}), bf16[32,4,512]{2,1,0:T(4,128)(2,1)S(1)}, u32[]{:S(2)}, u32[]{:S(2)}) async-start(bf16[32,4,512]{2,1,0:T(4,128)(2,1)} %reshape.566), calls=%async_computation.2 | async-start | bytes 262144 | tf_op jit(solution)/shard_map/all_to_all | solution.py:83
  121.4 20.8 %all-to-all-start.3 = ((bf16[32,4,512]{2,1,0:T(4,128)(2,1)}), bf16[32,4,512]{2,1,0:T(4,128)(2,1)S(1)}, u32[]{:S(2)}, u32[]{:S(2)}) async-start(bf16[32,4,512]{2,1,0:T(4,128)(2,1)} %reshape.590), calls=%async_computation.3 | async-start | bytes 262144 | tf_op jit(solution)/shard_map/all_to_all | solution.py:83
  172.2 23.3 %copy-start.6 = (f32[512,512]{1,0:T(8,128)S(1)}, f32[512,512]{1,0:T(8,128)}, u32[]{:S(2)}) copy-start(f32[512,512]{1,0:T(8,128)} %scatter_custom_fusion.3) | copy-start | bytes 3145732
  177.0 33.6 %copy-start.12 = (bf16[512,512]{1,0:T(8,128)(2,1)S(1)}, bf16[512,512]{1,0:T(8,128)(2,1)}, u32[]{:S(2)}) copy-start(bf16[512,512]{1,0:T(8,128)(2,1)} %param.17) | copy-start | bytes 1572868
  189.7 22.5 %all-to-all-start.4 = ((bf16[32,4,512]{2,1,0:T(4,128)(2,1)}), bf16[32,4,512]{2,1,0:T(4,128)(2,1)S(1)}, u32[]{:S(2)}, u32[]{:S(2)}) async-start(bf16[32,4,512]{2,1,0:T(4,128)(2,1)} %reshape.509), calls=%async_computation.4 | async-start | bytes 262144 | tf_op jit(solution)/shard_map/all_to_all | solution.py:83
  225.8 31.9 %copy-start.36 = (bf16[128,512]{1,0:T(8,128)(2,1)S(1)}, bf16[128,512]{1,0:T(8,128)(2,1)}, u32[]{:S(2)}) copy-start(bf16[128,512]{1,0:T(8,128)(2,1)} %copy-done.35) | copy-start | bytes 393220
  230.3 28.7 %copy-start.19 = (f32[1,512,512]{1,2,0:T(8,128)S(1)}, f32[1,512,512]{1,2,0:T(8,128)}, u32[]{:S(2)}) copy-start(f32[1,512,512]{1,2,0:T(8,128)} %convolution_bitcast_fusion) | copy-start | bytes 3145732
  251.7 14.1 %all-to-all-start.5 = ((bf16[32,4,512]{2,1,0:T(4,128)(2,1)}), bf16[32,4,512]{2,1,0:T(4,128)(2,1)}, u32[]{:S(2)}, u32[]{:S(2)}) async-start(bf16[32,4,512]{2,1,0:T(4,128)(2,1)} %reshape.510), calls=%async_computation.5 | async-start | bytes 262144 | tf_op jit(solution)/shard_map/all_to_all | solution.py:83
  279.9 30.0 %copy-start.34 = (bf16[128,512]{1,0:T(8,128)(2,1)S(1)}, bf16[128,512]{1,0:T(8,128)(2,1)}, u32[]{:S(2)}) copy-start(bf16[128,512]{1,0:T(8,128)(2,1)} %copy-done.33) | copy-start | bytes 393220
  284.4 26.8 %copy-start.17 = (f32[1,512,512]{1,2,0:T(8,128)S(1)}, f32[1,512,512]{1,2,0:T(8,128)}, u32[]{:S(2)}) copy-start(f32[1,512,512]{1,2,0:T(8,128)} %convolution_bitcast_fusion.3) | copy-start | bytes 3145732
  305.9 12.2 %all-to-all-start.6 = ((bf16[32,4,512]{2,1,0:T(4,128)(2,1)}), bf16[32,4,512]{2,1,0:T(4,128)(2,1)}, u32[]{:S(2)}, u32[]{:S(2)}) async-start(bf16[32,4,512]{2,1,0:T(4,128)(2,1)} %reshape.511), calls=%async_computation.6 | async-start | bytes 262144 | tf_op jit(solution)/shard_map/all_to_all | solution.py:83
  332.0 29.8 %copy-start.38 = (bf16[128,512]{1,0:T(8,128)(2,1)S(1)}, bf16[128,512]{1,0:T(8,128)(2,1)}, u32[]{:S(2)}) copy-start(bf16[128,512]{1,0:T(8,128)(2,1)} %param.18) | copy-start | bytes 393220
  332.0 31.2 %copy-start.61 = (f32[512]{0:T(512)S(1)}, f32[512]{0:T(512)}, u32[]{:S(2)}) copy-start(f32[512]{0:T(512)} %get-tuple-element.9) | copy-start | bytes 6148
  332.0 31.1 %copy-start.62 = (f32[512]{0:T(512)S(1)}, f32[512]{0:T(512)}, u32[]{:S(2)}) copy-start(f32[512]{0:T(512)} %get-tuple-element.16) | copy-start | bytes 6148
  336.4 27.4 %copy-start.16 = (f32[1,512,512]{1,2,0:T(8,128)S(1)}, f32[1,512,512]{1,2,0:T(8,128)}, u32[]{:S(2)}) copy-start(f32[1,512,512]{1,2,0:T(8,128)} %convolution_bitcast_fusion.6) | copy-start | bytes 3145732
  336.4 27.5 %copy-start.18 = (f32[1,512,512]{1,2,0:T(8,128)S(1)}, f32[1,512,512]{1,2,0:T(8,128)}, u32[]{:S(2)}) copy-start(f32[1,512,512]{1,2,0:T(8,128)} %convolution_bitcast_fusion.7) | copy-start | bytes 3145732
  357.9 12.1 %all-to-all-start.7 = ((bf16[32,4,512]{2,1,0:T(4,128)(2,1)}), bf16[32,4,512]{2,1,0:T(4,128)(2,1)S(1)}, u32[]{:S(2)}, u32[]{:S(2)}) async-start(bf16[32,4,512]{2,1,0:T(4,128)(2,1)} %reshape.512), calls=%async_computation.7 | async-start | bytes 262144 | tf_op jit(solution)/shard_map/all_to_all | solution.py:83
  (62 other events, 515.4 us)
where the time goes:
time: 613 us; the launch traced here: 602 us
  blocking collectives  211 us (34%)
  other arithmetic  192 us (31%)
  local copies, waits for them, and re-layouts  95.8 us (16%)
  matrix products  48.4 us (8%)
  starting transfers between devices  43.1 us (7%)
  waiting for transfers between devices  8.05 us (1%)
    psum x1, blocking collectives, shards(): lax.psum((weight_stack, gain_stack), ('lat', 'lon'))  211 us
    scatter-add x4, other arithmetic, edge_forward(): jax.ops.segment_sum(hidden, receivers, num_segments=proj_recv.shape[0])  48.4 us
    all_to_all x8, starting transfers between devices, trade(): lax.all_to_all(buffer, ('lat', 'lon'), split_axis=0, concat_axis=0, tiled...  43.1 us
    scatter-add x4, other arithmetic, edge_backward(): jax.ops.segment_sum(grad_pre, senders, num_segments=slot_count)  41.9 us
    scatter-add x4, other arithmetic, edge_backward(): jax.ops.segment_sum(grad_pre, receivers, num_segments=recv_count)  41.7 us
    gather x4, local copies, waits for them, and re-layouts, edge_forward(): slot_vals[senders].astype(jnp.float32)  22 us
    gather x4, local copies, waits for them, and re-layouts, edge_forward(): proj_recv[receivers].astype(jnp.float32)  21.1 us
    unnamed x163, local copies, waits for them, and re-layouts  20.5 us
  transfers between devices with their start and end apart: 8, of which 5 were waited for; matrix products, arithmetic and copies ran while one was open for 13% of the time, Pallas kernels for 0%

commit v1 on v0

--- a/solution.py
+++ b/solution.py
@@ -6,6 +6,11 @@
 LAYERS = 2
 EDGE_BLOCK = 128
 EPSILON = 1e-05
+
+
+def axis_by_axis(x, inner_axis, outer_axis):
+    half = lax.psum(x, inner_axis)
+    return lax.psum(half, outer_axis)
 
 
 def silu_slope(values):
@@ -215,7 +220,7 @@
     weight_parts[0], gain_parts[0] = settle(grad_weights, gain_part)
     weight_stack = jnp.stack(weight_parts)
     gain_stack = jnp.stack(gain_parts)
-    weight_stack, gain_stack = lax.psum((weight_stack, gain_stack), ("lat", "lon"))
+    weight_stack, gain_stack = axis_by_axis((weight_stack, gain_stack), "lat", "lon")
     return (grid_out, weight_stack.astype(jnp.bfloat16), gain_stack)
 
 

time: 613 us -> 1090 us (1.78)
  waiting for transfers between devices: 8.05 us -> 420 us
  blocking collectives: 211 us -> 261 us
  between operations: 4.38 us -> 17.7 us
    psum x0 -> x1, waiting for transfers between devices: none -> 412 us  [axis_by_axis(): half = lax.psum(x, inner_axis)]
    psum x1 -> x2, blocking collectives: 211 us -> 261 us  [the longest x1 250 us: axis_by_axis(): return lax.psum(half, outer_axis)]
  transfers between devices with their start and end apart: 8 -> 9, of which waited for: 5 -> 6; matrix products, arithmetic and copies ran while one was open for 13% -> 7% of each run, Pallas kernels for 0% -> 0%
where the time goes in v1:
time: 1090 us; the launch traced here: 1080 us
  waiting for transfers between devices  420 us (39%)
  blocking collectives  261 us (24%)
  other arithmetic  191 us (18%)
  local copies, waits for them, and re-layouts  95.7 us (9%)
  matrix products  48.4 us (4%)
  starting transfers between devices  43.1 us (4%)
  between operations  17.7 us (2%)
    psum x1, waiting for transfers between devices, axis_by_axis(): half = lax.psum(x, inner_axis)  412 us
    psum x1, blocking collectives, axis_by_axis(): return lax.psum(half, outer_axis)  250 us
    scatter-add x4, other arithmetic, edge_forward(): jax.ops.segment_sum(hidden, receivers, num_segments=proj_recv.shape[0])  48.4 us
    all_to_all x8, starting transfers between devices, trade(): lax.all_to_all(buffer, ('lat', 'lon'), split_axis=0, concat_axis=0, tiled...  43.1 us
    scatter-add x4, other arithmetic, edge_backward(): jax.ops.segment_sum(grad_pre, senders, num_segments=slot_count)  41.9 us
    scatter-add x4, other arithmetic, edge_backward(): jax.ops.segment_sum(grad_pre, receivers, num_segments=recv_count)  41.7 us
    gather x4, local copies, waits for them, and re-layouts, edge_forward(): slot_vals[senders].astype(jnp.float32)  22 us
  transfers between devices with their start and end apart: 9, of which 6 were waited for; matrix products, arithmetic and copies ran while one was open for 7% of the time, Pallas kernels for 0%

profile of v1, /device:TPU:0, one launch (start us, length us, event | category | flops | bytes accessed | tf_op | source)
XLA Modules:
  0.0 1077.7 jit_solution(8732760198592500848)
XLA Ops:
  11.4 7.3 all-to-all-start
  37.7 11.8 %scatter_custom_fusion = f32[128,512]{1,0:T(8,128)S(1)} fusion(s32[1536]{0:T(1024)S(1)} %reduce.1, bf16[1536,512]{1,0:T(8,128)(2,1)S(1)} %gather_fusion.2, bf16[1536,512]{1,0:T(8,128)(2,1)} %gather_fusion.1, f32[1536]{0:T(1024)S(1)} %fusion.133, f32[]{:T(128)} %constant.63.clone.1, f32[]{:T(128)} %constant.59.clone.1), kind=kCustom, calls=%fused_computation.56 | custom fusion | flops 7077888 | bytes 3416072 | tf_op jit(solution)/shard_map/scatter-add | solution.py:42
  54.8 5.8 all-to-all-start.1
  62.7 5.4 gather_fusion.5
  74.3 11.9 %scatter_custom_fusion.1 = f32[128,512]{1,0:T(8,128)S(1)} fusion(s32[1536]{0:T(1024)S(1)} %reduce.4, bf16[1536,512]{1,0:T(8,128)(2,1)} %gather_fusion.5, bf16[1536,512]{1,0:T(8,128)(2,1)} %gather_fusion.4, f32[1536]{0:T(1024)S(1)} %fusion.134, f32[]{:T(128)} %constant.63.clone.1, f32[]{:T(128)} %constant.59.clone.1), kind=kCustom, calls=%fused_computation.51 | custom fusion | flops 7077888 | bytes 3416072 | tf_op jit(solution)/shard_map/scatter-add | solution.py:42
  104.9 5.4 gather_fusion.7
  110.3 11.7 %scatter_custom_fusion.2 = f32[128,512]{1,0:T(8,128)S(1)} fusion(s32[1536]{0:T(1024)S(1)} %reduce.4, bf16[1536,512]{1,0:T(8,128)(2,1)} %gather_fusion.8, bf16[1536,512]{1,0:T(8,128)(2,1)} %gather_fusion.7, f32[1536]{0:T(1024)S(1)} %fusion.134, f32[]{:T(128)} %constant.63.clone.1, f32[]{:T(128)} %constant.59.clone.1), kind=kCustom, calls=%fused_computation.46 | custom fusion | flops 7077888 | bytes 3416072 | tf_op jit(solution)/shard_map/scatter-add | solution.py:42
  148.8 5.7 gather_fusion.10
  154.5 13.0 %scatter_custom_fusion.3 = f32[512,512]{1,0:T(8,128)} fusion(s32[1536]{0:T(1024)} %reduce, bf16[1536,512]{1,0:T(8,128)(2,1)S(1)} %copy-done.3, bf16[1536,512]{1,0:T(8,128)(2,1)} %gather_fusion.10, f32[1536]{0:T(1024)} %fusion.135, f32[]{:T(128)} %constant.63.clone.1, f32[]{:T(128)} %constant.59.clone.1), kind=kCustom, calls=%fused_computation.41 | custom fusion | flops 7077888 | bytes 4203520 | tf_op jit(solution)/shard_map/scatter-add | solution.py:42
  183.5 11.0 %scatter_custom_fusion.4 = f32[128,512]{1,0:T(8,128)} fusion(s32[1536]{0:T(1024)} %reduce.10, f32[1536,512]{1,0:T(8,128)} %multiply_multiply_fusion.3, f32[]{:T(128)} %constant.59.clone.1), kind=kCustom, calls=%fused_computation.206 | custom fusion | flops 786432 | bytes 262656 | tf_op jit(solution)/shard_map/scatter-add | solution.py:81
  196.1 5.8 all-to-all-start.4
  204.6 10.5 scatter_custom_fusion.15
  234.8 10.4 scatter_custom_fusion.6
  245.2 10.3 scatter_custom_fusion.7
  256.2 6.0 all-to-all-start.5
  288.9 10.4 scatter_custom_fusion.9
  299.3 10.3 scatter_custom_fusion.10
  340.9 10.5 scatter_custom_fusion.14
  351.4 10.3 scatter_custom_fusion.12
  380.4 6.7 pad_maximum_fusion
  389.2 10.7 psum.30
  399.9 411.7 %all-reduce.4.cloned.1.call-done = f32[4,3,512,512]{2,3,1,0:T(8,128)} async-done(((f32[4,3,512,512]{2,3,1,0:T(8,128)}), f32[4,3,512,512]{2,3,1,0:T(8,128)}) %all-reduce.4.cloned.1.call-update) | async-done | bytes 12582928 | tf_op jit(solution)/shard_map/psum | solution.py:12
  811.6 250.3 %all-reduce.5 = (bf16[4,3,512,512]{2,3,1,0:T(8,128)(2,1)}, f32[4,512]{1,0:T(4,128)}) all-reduce(f32[4,3,512,512]{2,3,1,0:T(8,128)} %all-reduce.4.cloned.1.call-done, f32[4,512]{1,0:T(4,128)S(1)} %psum.30), channel_id=1, replica_groups=mesh['lat'=4,'lon'=8] {'lon'}, use_global_device_ids=true, to_apply=%region_33.34 | all-reduce | flops 3147776 | bytes 18890752 | tf_op jit(solution)/shard_map/psum | solution.py:13
  1061.8 8.6 copy.57
  (328 shorter events, 198.5 us)
Async XLA Ops:
  11.4 20.8 %all-to-all-start = ((bf16[32,4,512]{2,1,0:T(4,128)(2,1)}), bf16[32,4,512]{2,1,0:T(4,128)(2,1)S(1)}, u32[]{:S(2)}, u32[]{:S(2)}) async-start(bf16[32,4,512]{2,1,0:T(4,128)(2,1)} %reshape.518), calls=%async_computation | async-start | bytes 262144 | tf_op jit(solution)/shard_map/all_to_all | solution.py:88
  23.1 28.1 %copy-start.49 = (f32[1,512]{1,0:T(1,128)}, f32[1,512]{1,0:T(1,128)S(1)}, u32[]{:S(2)}) copy-start(f32[1,512]{1,0:T(1,128)S(1)} %get-tuple-element.27) | copy-start | bytes 6148
  23.1 64.8 %copy-start.51 = (f32[1,512]{1,0:T(1,128)}, f32[1,512]{1,0:T(1,128)S(1)}, u32[]{:S(2)}) copy-start(f32[1,512]{1,0:T(1,128)S(1)} %get-tuple-element.26) | copy-start | bytes 6148
  51.9 36.0 %copy-start.34 = (bf16[128,512]{1,0:T(8,128)(2,1)}, bf16[128,512]{1,0:T(8,128)(2,1)S(1)}, u32[]{:S(2)}) copy-start(bf16[128,512]{1,0:T(8,128)(2,1)S(1)} %add_convert_fusion.3) | copy-start | bytes 393220
  54.8 14.0 %all-to-all-start.1 = ((bf16[32,4,512]{2,1,0:T(4,128)(2,1)}), bf16[32,4,512]{2,1,0:T(4,128)(2,1)S(1)}, u32[]{:S(2)}, u32[]{:S(2)}) async-start(bf16[32,4,512]{2,1,0:T(4,128)(2,1)} %reshape.542), calls=%async_computation.1 | async-start | bytes 262144 | tf_op jit(solution)/shard_map/all_to_all | solution.py:88
  61.2 49.1 %copy-start.71 = (s32[1536]{0:T(1024)}, s32[1536]{0:T(1024)S(1)}, u32[]{:S(2)}) copy-start(s32[1536]{0:T(1024)S(1)} %reduce.4) | copy-start | bytes 18436
  88.6 35.1 %copy-start.36 = (bf16[128,512]{1,0:T(8,128)(2,1)}, bf16[128,512]{1,0:T(8,128)(2,1)S(1)}, u32[]{:S(2)}) copy-start(bf16[128,512]{1,0:T(8,128)(2,1)S(1)} %add_convert_fusion.2) | copy-start | bytes 393220
  91.5 13.4 %all-to-all-start.2 = ((bf16[32,4,512]{2,1,0:T(4,128)(2,1)}), bf16[32,4,512]{2,1,0:T(4,128)(2,1)S(1)}, u32[]{:S(2)}, u32[]{:S(2)}) async-start(bf16[32,4,512]{2,1,0:T(4,128)(2,1)} %reshape.566), calls=%async_computation.2 | async-start | bytes 262144 | tf_op jit(solution)/shard_map/all_to_all | solution.py:88
  122.0 20.7 %copy-start.30 = (f32[128,512]{1,0:T(8,128)}, f32[128,512]{1,0:T(8,128)S(1)}, u32[]{:S(2)}) copy-start(f32[128,512]{1,0:T(8,128)S(1)} %scatter_custom_fusion.2) | copy-start | bytes 786436
  127.9 20.8 %all-to-all-start.3 = ((bf16[32,4,512]{2,1,0:T(4,128)(2,1)}), bf16[32,4,512]{2,1,0:T(4,128)(2,1)S(1)}, u32[]{:S(2)}, u32[]{:S(2)}) async-start(bf16[32,4,512]{2,1,0:T(4,128)(2,1)} %reshape.590), calls=%async_computation.3 | async-start | bytes 262144 | tf_op jit(solution)/shard_map/all_to_all | solution.py:88
  178.7 23.3 %copy-start.6 = (f32[512,512]{1,0:T(8,128)S(1)}, f32[512,512]{1,0:T(8,128)}, u32[]{:S(2)}) copy-start(f32[512,512]{1,0:T(8,128)} %scatter_custom_fusion.3) | copy-start | bytes 3145732
  183.5 31.5 %copy-start.12 = (bf16[512,512]{1,0:T(8,128)(2,1)S(1)}, bf16[512,512]{1,0:T(8,128)(2,1)}, u32[]{:S(2)}) copy-start(bf16[512,512]{1,0:T(8,128)(2,1)} %param.17) | copy-start | bytes 1572868
  196.1 20.4 %all-to-all-start.4 = ((bf16[32,4,512]{2,1,0:T(4,128)(2,1)}), bf16[32,4,512]{2,1,0:T(4,128)(2,1)S(1)}, u32[]{:S(2)}, u32[]{:S(2)}) async-start(bf16[32,4,512]{2,1,0:T(4,128)(2,1)} %reshape.509), calls=%async_computation.4 | async-start | bytes 262144 | tf_op jit(solution)/shard_map/all_to_all | solution.py:88
  230.2 31.9 %copy-start.37 = (bf16[128,512]{1,0:T(8,128)(2,1)S(1)}, bf16[128,512]{1,0:T(8,128)(2,1)}, u32[]{:S(2)}) copy-start(bf16[128,512]{1,0:T(8,128)(2,1)} %copy-done.36) | copy-start | bytes 393220
  234.8 28.8 %copy-start.19 = (f32[1,512,512]{1,2,0:T(8,128)S(1)}, f32[1,512,512]{1,2,0:T(8,128)}, u32[]{:S(2)}) copy-start(f32[1,512,512]{1,2,0:T(8,128)} %convolution_bitcast_fusion) | copy-start | bytes 3145732
  256.2 14.1 %all-to-all-start.5 = ((bf16[32,4,512]{2,1,0:T(4,128)(2,1)}), bf16[32,4,512]{2,1,0:T(4,128)(2,1)}, u32[]{:S(2)}, u32[]{:S(2)}) async-start(bf16[32,4,512]{2,1,0:T(4,128)(2,1)} %reshape.510), calls=%async_computation.5 | async-start | bytes 262144 | tf_op jit(solution)/shard_map/all_to_all | solution.py:88
  284.3 30.1 %copy-start.35 = (bf16[128,512]{1,0:T(8,128)(2,1)S(1)}, bf16[128,512]{1,0:T(8,128)(2,1)}, u32[]{:S(2)}) copy-start(bf16[128,512]{1,0:T(8,128)(2,1)} %copy-done.34) | copy-start | bytes 393220
  288.9 26.8 %copy-start.17 = (f32[1,512,512]{1,2,0:T(8,128)S(1)}, f32[1,512,512]{1,2,0:T(8,128)}, u32[]{:S(2)}) copy-start(f32[1,512,512]{1,2,0:T(8,128)} %convolution_bitcast_fusion.3) | copy-start | bytes 3145732
  310.3 12.3 %all-to-all-start.6 = ((bf16[32,4,512]{2,1,0:T(4,128)(2,1)}), bf16[32,4,512]{2,1,0:T(4,128)(2,1)}, u32[]{:S(2)}, u32[]{:S(2)}) async-start(bf16[32,4,512]{2,1,0:T(4,128)(2,1)} %reshape.511), calls=%async_computation.6 | async-start | bytes 262144 | tf_op jit(solution)/shard_map/all_to_all | solution.py:88
  336.5 29.8 %copy-start.39 = (bf16[128,512]{1,0:T(8,128)(2,1)S(1)}, bf16[128,512]{1,0:T(8,128)(2,1)}, u32[]{:S(2)}) copy-start(bf16[128,512]{1,0:T(8,128)(2,1)} %param.18) | copy-start | bytes 393220
  340.9 26.8 %copy-start.16 = (f32[1,512,512]{1,2,0:T(8,128)S(1)}, f32[1,512,512]{1,2,0:T(8,128)}, u32[]{:S(2)}) copy-start(f32[1,512,512]{1,2,0:T(8,128)} %convolution_bitcast_fusion.6) | copy-start | bytes 3145732
  340.9 26.8 %copy-start.18 = (f32[1,512,512]{1,2,0:T(8,128)S(1)}, f32[1,512,512]{1,2,0:T(8,128)}, u32[]{:S(2)}) copy-start(f32[1,512,512]{1,2,0:T(8,128)} %convolution_bitcast_fusion.7) | copy-start | bytes 3145732
  362.4 12.1 %all-to-all-start.7 = ((bf16[32,4,512]{2,1,0:T(4,128)(2,1)}), bf16[32,4,512]{2,1,0:T(4,128)(2,1)S(1)}, u32[]{:S(2)}, u32[]{:S(2)}) async-start(bf16[32,4,512]{2,1,0:T(4,128)(2,1)} %reshape.512), calls=%async_computation.7 | async-start | bytes 262144 | tf_op jit(solution)/shard_map/all_to_all | solution.py:88
  366.3 445.2 %all-reduce.4.cloned.1.call-start = ((), (), s32[]{:S(2)}) async-start(), calls=%async_computation.8 | async-start | bytes 25165824 | tf_op jit(solution)/shard_map/psum | solution.py:12
  (66 other events, 505.2 us)
Sparse Core Ops, SparseCore 0:
  387.2 424.2 all-reduce.3
